TPU v7x, 8 devices: a whole 2x2x1 slice. The times are simulated.
8 devices in a mesh: rep: 2 (over y, z), dp: 4 (over x, core).
Axes of the slice: x: 2, y: 2, z: 1, core: 2. Of those that a mesh axis runs over, the one named last changes fastest.
Arguments:
- a: bfloat16 [8, 4, 4096, 1024], P(('rep', 'dp')), parts along dimension 0
- g: bfloat16 [8, 4, 4096, 3200], P(('rep', 'dp')), parts along dimension 0
Outputs:
- output: bfloat16 [8, 1024, 3200], P('rep'), parts along dimension 0
There are 2 independent parts. A program takes and returns all parts, laid end to end along the dimension named above; each array names one.
All inputs are finite; a program needn't handle non-finite values.
Results may differ from a plain program's by a relative error of at most 0.012.
Values are sent between devices in bfloat16 or wider.
A program may use at most 2 GiB of HBM per device.

v0:
```python
import jax
import jax.numpy as jnp


def solution(mesh):
    groups = mesh.shape["rep"]

    def step(a, g):
        a, g = (t.reshape(groups, -1, *t.shape[1:]) for t in (a, g))
        sums = jnp.einsum("rsntd,rsntf->rndf", a, g, preferred_element_type=jnp.float32)
        return sums.astype(jnp.bfloat16).reshape(-1, *sums.shape[2:])

    return step
```

profile of v0, /device:TPU:0, one launch (start us, length us, event | category | flops | bytes accessed | tf_op | source)
XLA Modules:
  0.0 1012.5 jit_solution(2056453160593247383)
XLA Ops:
  0.0 128.3 %fusion.2 = f32[1,4,1024,3200]{3,2,1,0:T(8,128)} fusion(bf16[1,4,4096,3200]{3,2,1,0:T(8,128)(2,1)} %param.1, bf16[1,4,4096,1024]{3,2,1,0:T(8,128)(2,1)} %param), kind=kOutput, calls=%fused_computation.2 | convolution fusion | flops 107374182400 | bytes 190840832 | tf_op jit(solution)/rsntd,rsntf->rndf/dot_general | solution.py:10
  128.3 884.2 %all-reduce.2 = bf16[1,4,1024,3200]{3,2,1,0:T(8,128)(2,1)} all-reduce(f32[1,4,1024,3200]{3,2,1,0:T(8,128)} %fusion.2), channel_id=1, replica_groups=[2,4]<=[8], use_global_device_ids=true, to_apply=%add.clone | all-reduce | flops 13107200 | bytes 78643200 | tf_op jit(solution)/rsntd,rsntf->rndf/dot_general | solution.py:10
where the time goes:
time: 1010 us
  blocking collectives  884 us (88%)
  matrix products  128 us (13%)
    dot_general x1, blocking collectives, step(): jnp.einsum('rsntd,rsntf->rndf', a, g, preferred_element_type=jnp.float32)  884 us
    dot_general x1, matrix products, step(): jnp.einsum('rsntd,rsntf->rndf', a, g, preferred_element_type=jnp.float32)  128 us

commit v1 on v0

v1 whole, which is shorter than its diff:
```python
import functools

import jax
import jax.numpy as jnp
from jax import lax
from jax.experimental import pallas as pl
from jax.experimental.pallas import tpu as pltpu
from jax.sharding import PartitionSpec as P

MESH = pl.DeviceIdType.MESH
WIDTH = 640
LAG = 2
LAG2 = 2 * LAG + 1
RING = 4


def kernel(
    a, g, out, abuf, gbuf, sb1, rv1, mine, sb2, rv2, fin,
    asem, gsem, s1, r1, s2, r2, local, s3, r3, s4, r4, s5, r5,
):
    _, mats, tokens, dim = a.shape
    quarter = dim // 4
    per = g.shape[3] // WIDTH
    chunks = mats * per
    rep, dp = lax.axis_index("rep"), lax.axis_index("dp")
    partner = 2 * (dp // 2) + 1 - dp % 2
    peer = (dp + 2) % 4
    peers_partner = 3 - dp
    order = (peers_partner, partner, peer, dp)

    def rows(q):
        return pl.ds(pl.multiple_of(q * quarter, quarter), quarter)

    def place(k, q):
        return out.at[k // per, rows(q), pl.ds(pl.multiple_of((k % per) * WIDTH, 128), WIDTH)]

    def load_a(n, i):
        return pltpu.make_async_copy(
            a.at[0, n, :, rows(order[i])], abuf.at[n % 2, :, rows(order[i])], asem.at[n % 2, i])

    def load_g(k):
        cols = pl.ds(pl.multiple_of((k % per) * WIDTH, 128), WIDTH)
        return pltpu.make_async_copy(g.at[0, k // per, :, cols], gbuf.at[k % 2], gsem.at[k % 2])

    def remote(src, dst, send, recv, to):
        return pltpu.make_async_remote_copy(
            src_ref=src, dst_ref=dst, send_sem=send, recv_sem=recv,
            device_id=(rep, to), device_id_type=MESH)

    def term(k, i):
        return remote(sb1.at[k % 2, i], rv1.at[k, i], s1.at[k % 2, i], r1.at[k, i], partner)

    def half(k):
        return remote(sb2.at[k % RING], rv2.at[k], s2.at[k % RING], r2.at[k], peer)

    def keep(k):
        return pltpu.make_async_copy(fin.at[k % RING], place(k, dp), local.at[k % RING])

    def give(k):
        return remote(fin.at[k % RING], place(k, dp), s3.at[k % RING], r3.at[k], partner)

    def cross(k):
        return remote(fin.at[k % RING], place(k, dp), s4.at[k % RING], r4.at[k], peer)

    def forward(k):
        return remote(place(k, peer), place(k, peer), s5.at[k], r5.at[k], partner)

    def product(k, i):
        left = abuf[(k // per) % 2, :, rows(order[i])]
        return lax.dot_general(left, gbuf[k % 2], (((0,), (0,)), ((), ())), preferred_element_type=jnp.float32)

    def multiply(k):
        n = k // per
        first = k % per == 0

        @pl.when(k + 1 < chunks)
        def _():
            load_g(k + 1).start()

        @pl.when(first & (n + 1 < mats))
        def _():
            for i in range(4):
                load_a(n + 1, i).start()

        load_g(k).wait()

        def ready(i):
            @pl.when(first)
            def _():
                load_a(n, i).wait()

        for i in range(2):
            @pl.when(k >= 2)
            def _():
                term(k - 2, i).wait_send()

            ready(i)
            sb1[k % 2, i] = product(k, i).astype(jnp.bfloat16)
            term(k, i).start()
        ready(2)
        total = product(k, 2)
        term(k, 0).wait_recv()

        @pl.when(k >= RING)
        def _():
            half(k - RING).wait_send()

        sb2[k % RING] = (total + rv1[k, 0].astype(jnp.float32)).astype(jnp.bfloat16)
        half(k).start()
        ready(3)
        total = product(k, 3)
        term(k, 1).wait_recv()
        mine[k % (LAG + 1)] = total + rv1[k, 1].astype(jnp.float32)

    def finish(k):
        half(k).wait_recv()

        @pl.when(k >= RING)
        def _():
            keep(k - RING).wait()
            give(k - RING).wait_send()
            cross(k - RING).wait_send()

        fin[k % RING] = (mine[k % (LAG + 1)] + rv2[k].astype(jnp.float32)).astype(jnp.bfloat16)
        cross(k).start()
        give(k).start()
        keep(k).start()

    def hand_on(k):
        cross(k).wait_recv()
        forward(k).start()

    load_a(0, 0).start()
    load_g(0).start()
    for i in range(1, 4):
        load_a(0, i).start()
    barrier = pltpu.get_barrier_semaphore()
    for other in (partner, peer):
        pl.semaphore_signal(barrier, inc=1, device_id=(rep, other), device_id_type=MESH)
    pl.semaphore_wait(barrier, 2)

    def step(k, _):
        @pl.when(k < chunks)
        def _():
            multiply(k)

        @pl.when((k >= LAG) & (k < chunks + LAG))
        def _():
            finish(k - LAG)

        @pl.when(k >= LAG2)
        def _():
            hand_on(k - LAG2)

    lax.fori_loop(0, chunks + LAG2, step, None)

    def drain(k, _):
        give(k).wait_recv()
        forward(k).wait()

    for k in range(chunks - 2, chunks):
        for i in range(2):
            term(k, i).wait_send()
    for k in range(chunks - RING, chunks):
        half(k).wait_send()
        keep(k).wait()
        give(k).wait_send()
        cross(k).wait_send()
    lax.fori_loop(0, chunks, drain, None)


def solution(mesh):
    def step(a, g):
        _, mats, tokens, dim = a.shape
        wide = g.shape[3]
        chunks = mats * (wide // WIDTH)
        block = (dim // 4, WIDTH)
        dma = pltpu.SemaphoreType.DMA
        bf16, f32 = jnp.bfloat16, jnp.float32
        return pl.pallas_call(
            kernel,
            out_shape=jax.ShapeDtypeStruct((mats, dim, wide), bf16),
            in_specs=[pl.BlockSpec(memory_space=pl.ANY)] * 2,
            out_specs=pl.BlockSpec(memory_space=pl.ANY),
            scratch_shapes=[
                pltpu.VMEM((2, tokens, dim), bf16),
                pltpu.VMEM((2, tokens, WIDTH), bf16),
                pltpu.VMEM((2, 2, *block), bf16),
                pltpu.VMEM((chunks, 2, *block), bf16),
                pltpu.VMEM((LAG + 1, *block), f32),
                pltpu.VMEM((RING, *block), bf16),
                pltpu.VMEM((chunks, *block), bf16),
                pltpu.VMEM((RING, *block), bf16),
                dma((2, 4)), dma((2,)),
                dma((2, 2)), dma((chunks, 2)),
                dma((RING,)), dma((chunks,)),
                dma((RING,)),
                dma((RING,)), dma((chunks,)),
                dma((RING,)), dma((chunks,)),
                dma((chunks,)), dma((chunks,)),
            ],
            compiler_params=pltpu.CompilerParams(
                collective_id=0, has_side_effects=True, vmem_limit_bytes=66_000_000),
        )(a, g)

    both = P(("rep", "dp"))
    return jax.shard_map(step, mesh=mesh, in_specs=(both, both), out_specs=P("rep"), check_vma=False)
```

time: 1010 us -> 319 us (0.32)
  blocking collectives: 884 us -> 0 us
  Pallas kernels: 0 us -> 301 us
  matrix products: 128 us -> 0 us
  local copies, waits for them, and re-layouts: 0 us -> 18 us
    dot_general x1 -> x0, blocking collectives: 884 us -> none  [step(): jnp.einsum('rsntd,rsntf->rndf', a, g, preferred_element_type=jnp.float32)]
    pallas_call x0 -> x1, Pallas kernels: none -> 301 us  [step(): pl.pallas_call(kernel, out_shape=jax.ShapeDtypeStruct((mats, dim, wide),...]
    dot_general x1 -> x0, matrix products: 128 us -> none  [step(): jnp.einsum('rsntd,rsntf->rndf', a, g, preferred_element_type=jnp.float32)]
    unnamed x0 -> x1, local copies, waits for them, and re-layouts: none -> 18 us
where the time goes in v1:
time: 319 us
  Pallas kernels  301 us (94%)
  local copies, waits for them, and re-layouts  18 us (6%)
    pallas_call x1, Pallas kernels, step(): pl.pallas_call(kernel, out_shape=jax.ShapeDtypeStruct((mats, dim, wide),...  301 us
    unnamed x1, local copies, waits for them, and re-layouts  18 us

profile of v1, /device:TPU:0, one launch (start us, length us, event | category | flops | bytes accessed | tf_op | source)
XLA Modules:
  0.0 318.7 jit_solution(12976669407805806470)
XLA Ops:
  0.0 300.7 %shard_map.28 = bf16[4,1024,3200]{2,1,0:T(8,128)(2,1)} custom-call(bf16[1,4,4096,1024]{3,2,1,0:T(8,128)(2,1)} %a.1, bf16[1,4,4096,3200]{3,2,1,0:T(8,128)(2,1)} %g.1), custom_call_target="tpu_custom_call" | custom-call | tf_op jit(solution)/shard_map/pallas_call | solution.py:180
  300.7 18.0 %copy.4 = bf16[4,1024,3200]{2,1,0:T(8,128)(2,1)} copy(bf16[4,1024,3200]{2,1,0:T(8,128)(2,1)} %shard_map.28) | data formatting | bytes 52428800

commit v2 on v0

v2 whole, which is shorter than its diff:
```python
import jax
import jax.numpy as jnp
from jax import lax
from jax.experimental import pallas as pl
from jax.experimental.pallas import tpu as pltpu
from jax.sharding import PartitionSpec as P

MESH = pl.DeviceIdType.MESH
WIDTH = 640
RING = 4
PIECES = ((0, 128, 0, 256), (128, 128, 0, 256), (0, 256, 256, 256), (0, 256, 512, 128))


def kernel(
    a, g, out, abuf, gbuf, sb1, rv1, total, sb2, rv2,
    asem, hsem, gsem, g0sem, s1, r1, p1, q1, s2, r2, p2, q2, s3, r3, s4, r4, s5, r5,
):
    _, mats, tokens, dim = a.shape
    quarter = dim // 4
    per = g.shape[3] // WIDTH
    chunks = mats * per
    rep, dp = lax.axis_index("rep"), lax.axis_index("dp")
    partner = 2 * (dp // 2) + 1 - dp % 2
    peer = (dp + 2) % 4
    order = (3 - dp, partner, peer, dp)

    def rows(q, start=0, size=quarter):
        return pl.ds(pl.multiple_of(q * quarter + start, 128), size)

    def columns(k):
        return pl.ds(pl.multiple_of((k % per) * WIDTH, 128), WIDTH)

    def place(k, q):
        return out.at[k, rows(q)]

    def load_a(n, i):
        return pltpu.make_async_copy(
            a.at[0, n, :, rows(order[i])], abuf.at[n % 2, :, rows(order[i])], asem.at[n % 2, i])

    def load_half(i, h):
        part = rows(order[i], h * 128, 128)
        return pltpu.make_async_copy(a.at[0, 0, :, part], abuf.at[0, :, part], hsem.at[i // 2, h])

    def load_g(k):
        return pltpu.make_async_copy(g.at[0, k // per, :, columns(k)], gbuf.at[k % 3], gsem.at[k % 3])

    def load_g0(j, start, size):
        part = pl.ds(start, size)
        return pltpu.make_async_copy(g.at[0, 0, :, part], gbuf.at[0, :, part], g0sem.at[j])

    def remote(src, dst, send, recv, to):
        return pltpu.make_async_remote_copy(
            src_ref=src, dst_ref=dst, send_sem=send, recv_sem=recv,
            device_id=(rep, to), device_id_type=MESH)

    def term(k, i):
        return remote(sb1.at[k % 2, i], rv1.at[k % 2, i], s1.at[k % 2, i], r1.at[k, i], partner)

    def term_piece(j):
        r, h, c, w = PIECES[j]
        part = (pl.ds(r, h), pl.ds(c, w))
        return remote(sb1.at[0, 0, *part], rv1.at[0, 0, *part], p1.at[j], q1.at[j], partner)

    def half(k):
        return remote(sb2.at[k % 2], rv2.at[k % RING], s2.at[k % 2], r2.at[k], peer)

    def half_piece(j):
        r, h, c, w = PIECES[j]
        part = (pl.ds(r, h), pl.ds(c, w))
        return remote(sb2.at[0, *part], rv2.at[0, *part], p2.at[j], q2.at[j], peer)

    def give(k):
        return remote(place(k, dp), place(k, dp), s3.at[k], r3.at[k], partner)

    def cross(k):
        return remote(place(k, dp), place(k, dp), s4.at[k], r4.at[k], peer)

    def forward(k):
        return remote(place(k, peer), place(k, peer), s5.at[k], r5.at[k], partner)

    def dot(left, right):
        return lax.dot_general(left, right, (((0,), (0,)), ((), ())), preferred_element_type=jnp.float32)

    def product(k, i):
        return dot(abuf[(k // per) % 2, :, rows(order[i])], gbuf[k % 3])

    def both(here, there):
        return here + there.astype(jnp.float32)

    def first_part():
        def piece(j, i):
            r, h, c, w = PIECES[j]
            return dot(abuf[0, :, rows(order[i], r, h)], gbuf[0, :, c:c + w])

        def send(j):
            r, h, c, w = PIECES[j]
            term_piece(j).wait_recv()
            sb2[0, r:r + h, c:c + w] = both(total[r:r + h, c:c + w], rv1[0, 0, r:r + h, c:c + w]).astype(jnp.bfloat16)
            half_piece(j).start()

        for j, (r, h, c, w) in enumerate(PIECES):
            if j == 0:
                load_half(0, 0).wait()
                load_g0(0, 0, 256).wait()
            if j == 1:
                load_half(0, 1).wait()
            if j == 2:
                load_g0(1, 256, 384).wait()
            sb1[0, 0, r:r + h, c:c + w] = piece(j, 0).astype(jnp.bfloat16)
            term_piece(j).start()
            if j:
                send(j - 1)
            if j < 2:
                load_half(2, j).wait()
            total[r:r + h, c:c + w] = piece(j, 2)
            if j == 0:
                load_g(1).start()
                load_a(0, 1).start()
                load_a(0, 3).start()
        send(len(PIECES) - 1)
        load_g(2).start()
        for i in range(4):
            load_a(1, i).start()

    def reduce_part(k):
        first = k % per == 0
        load_g(k).wait()

        @pl.when(first)
        def _():
            load_a(k // per, 0).wait()
            load_a(k // per, 2).wait()

        @pl.when(k == 2)
        def _():
            for j in range(len(PIECES)):
                term_piece(j).wait_send()

        @pl.when(k > 2)
        def _():
            term(k - 2, 0).wait_send()

        sb1[k % 2, 0] = product(k, 0).astype(jnp.bfloat16)
        term(k, 0).start()
        total[...] = product(k, 2)
        term(k, 0).wait_recv()

        @pl.when(k == 2)
        def _():
            for j in range(len(PIECES)):
                half_piece(j).wait_send()

        @pl.when(k > 2)
        def _():
            half(k - 2).wait_send()

        sb2[k % 2] = both(total[...], rv1[k % 2, 0]).astype(jnp.bfloat16)
        half(k).start()

    def owner_part(k):
        @pl.when(k % per == 0)
        def _():
            load_a(k // per, 1).wait()
            load_a(k // per, 3).wait()

        @pl.when(k >= 2)
        def _():
            term(k - 2, 1).wait_send()

        sb1[k % 2, 1] = product(k, 1).astype(jnp.bfloat16)
        term(k, 1).start()
        total[...] = product(k, 3)

        @pl.when(k + 3 < chunks)
        def _():
            load_g(k + 3).start()

        @pl.when((k % per == per - 1) & (k // per + 2 < mats))
        def _():
            for i in range(4):
                load_a(k // per + 2, i).start()

        term(k, 1).wait_recv()

        @pl.when(k == 0)
        def _():
            for j in range(len(PIECES)):
                half_piece(j).wait_recv()

        @pl.when(k > 0)
        def _():
            half(k).wait_recv()

        out[k, rows(dp)] = both(both(total[...], rv1[k % 2, 1]), rv2[k % RING]).astype(jnp.bfloat16)
        cross(k).start()
        give(k).start()

    load_half(0, 0).start()
    load_g0(0, 0, 256).start()
    load_half(2, 0).start()
    load_half(0, 1).start()
    load_half(2, 1).start()
    load_g0(1, 256, 384).start()
    barrier = pltpu.get_barrier_semaphore()
    for other in (partner, peer):
        pl.semaphore_signal(barrier, inc=1, device_id=(rep, other), device_id_type=MESH)
    pl.semaphore_wait(barrier, 2)
    first_part()

    def step(k, _):
        @pl.when(k + 1 < chunks)
        def _():
            reduce_part(k + 1)

        @pl.when(k < chunks)
        def _():
            owner_part(k)

        @pl.when(k >= 2)
        def _():
            cross(k - 2).wait_recv()
            forward(k - 2).start()

    lax.fori_loop(0, chunks + 2, step, None)

    for k in range(chunks - 2, chunks):
        for i in range(2):
            term(k, i).wait_send()
        half(k).wait_send()

    def drain(k, _):
        cross(k).wait_send()
        give(k).wait()
        forward(k).wait()

    lax.fori_loop(0, chunks, drain, None)


def write(done, out, sem):
    chunks = done.shape[0]
    per = chunks // out.shape[0]

    def copy(k):
        return pltpu.make_async_copy(done.at[k], out.at[k // per, :, pl.ds((k % per) * WIDTH, WIDTH)], sem.at[k])

    for k in range(chunks):
        copy(k).start()
    for k in range(chunks):
        copy(k).wait()


def solution(mesh):
    def step(a, g):
        _, mats, tokens, dim = a.shape
        wide = g.shape[3]
        chunks = mats * (wide // WIDTH)
        block = (dim // 4, WIDTH)
        dma = pltpu.SemaphoreType.DMA
        bf16, f32 = jnp.bfloat16, jnp.float32
        pieces = len(PIECES)
        done = pl.pallas_call(
            kernel,
            out_shape=pltpu.VMEM((chunks, dim, WIDTH), bf16),
            in_specs=[pl.BlockSpec(memory_space=pl.ANY)] * 2,
            out_specs=pl.BlockSpec(memory_space=pltpu.VMEM),
            scratch_shapes=[
                pltpu.VMEM((2, tokens, dim), bf16),
                pltpu.VMEM((3, tokens, WIDTH), bf16),
                pltpu.VMEM((2, 2, *block), bf16),
                pltpu.VMEM((2, 2, *block), bf16),
                pltpu.VMEM(block, f32),
                pltpu.VMEM((2, *block), bf16),
                pltpu.VMEM((RING, *block), bf16),
                dma((2, 4)), dma((2, 2)), dma((3,)), dma((2,)),
                dma((2, 2)), dma((chunks, 2)), dma((pieces,)), dma((pieces,)),
                dma((2,)), dma((chunks,)), dma((pieces,)), dma((pieces,)),
                dma((chunks,)), dma((chunks,)),
                dma((chunks,)), dma((chunks,)),
                dma((chunks,)), dma((chunks,)),
            ],
            compiler_params=pltpu.CompilerParams(
                collective_id=0, has_side_effects=True, vmem_limit_bytes=40_700_000),
            name="reduce",
        )(a, g)
        return pl.pallas_call(
            write,
            out_shape=jax.ShapeDtypeStruct((mats, dim, wide), bf16),
            in_specs=[pl.BlockSpec(memory_space=pltpu.VMEM)],
            out_specs=pl.BlockSpec(memory_space=pl.ANY),
            scratch_shapes=[dma((chunks,))],
            compiler_params=pltpu.CompilerParams(vmem_limit_bytes=1_000_000),
            name="write",
        )(done)

    both = P(("rep", "dp"))
    return jax.shard_map(step, mesh=mesh, in_specs=(both, both), out_specs=P("rep"), check_vma=False)
```

time: 1010 us -> 304 us (0.30)
  blocking collectives: 884 us -> 0 us
  Pallas kernels: 0 us -> 304 us
  matrix products: 128 us -> 0 us
    dot_general x1 -> x0, blocking collectives: 884 us -> none  [step(): jnp.einsum('rsntd,rsntf->rndf', a, g, preferred_element_type=jnp.float32)]
    pallas_call x0 -> x2, Pallas kernels: none -> 304 us  [the longest x1 295 us: step(): pl.pallas_call(kernel, out_shape=pltpu.VMEM((chunks, dim, WIDTH), bf16),...]
    dot_general x1 -> x0, matrix products: 128 us -> none  [step(): jnp.einsum('rsntd,rsntf->rndf', a, g, preferred_element_type=jnp.float32)]
where the time goes in v2:
time: 304 us
  Pallas kernels  304 us (100%)
    pallas_call x1, Pallas kernels, step(): pl.pallas_call(kernel, out_shape=pltpu.VMEM((chunks, dim, WIDTH), bf16),...  295 us
    pallas_call x1, Pallas kernels, step(): pl.pallas_call(write, out_shape=jax.ShapeDtypeStruct((mats, dim, wide), b...  8.87 us

profile of v2, /device:TPU:0, one launch (start us, length us, event | category | flops | bytes accessed | tf_op | source)
XLA Modules:
  0.0 303.7 jit_solution(13573659136235788802)
XLA Ops:
  0.0 294.6 %reduce.1.done = bf16[20,1024,640]{2,1,0:T(8,128)(2,1)S(1)} custom-call(bf16[1,4,4096,1024]{3,2,1,0:T(8,128)(2,1)} %a.1, bf16[1,4,4096,3200]{3,2,1,0:T(8,128)(2,1)} %g.1), custom_call_target="tpu_custom_call" | custom-call | tf_op jit(solution)/shard_map/reduce/pallas_call | solution.py:261
  294.6 8.9 %write.1 = bf16[4,1024,3200]{2,1,0:T(8,128)(2,1)} custom-call(bf16[20,1024,640]{2,1,0:T(8,128)(2,1)S(1)} %reduce.1.done), custom_call_target="tpu_custom_call" | custom-call | tf_op jit(solution)/shard_map/write/pallas_call | solution.py:285

commit v3 on v2

--- a/solution.py
+++ b/solution.py
@@ -1,3 +1,5 @@
+import functools
+
 import jax
 import jax.numpy as jnp
 from jax import lax
@@ -5,20 +7,24 @@
 from jax.experimental.pallas import tpu as pltpu
 from jax.sharding import PartitionSpec as P
 
+
 MESH = pl.DeviceIdType.MESH
 WIDTH = 640
 RING = 4
-PIECES = ((0, 128, 0, 256), (128, 128, 0, 256), (0, 256, 256, 256), (0, 256, 512, 128))
+PIECES = ((0, 128, 0, 256), (128, 128, 0, 256), (0, 256, 256, 384))
+LAST = 2
+TAIL = 128
 
 
 def kernel(
-    a, g, out, abuf, gbuf, sb1, rv1, total, sb2, rv2,
+    a, g, out, got, la, lb, abuf, gbuf, sb1, rv1, total, sb2, rv2,
     asem, hsem, gsem, g0sem, s1, r1, p1, q1, s2, r2, p2, q2, s3, r3, s4, r4, s5, r5,
 ):
-    _, mats, tokens, dim = a.shape
+    _, mats, _, dim = a.shape
     quarter = dim // 4
     per = g.shape[3] // WIDTH
     chunks = mats * per
+    inside = chunks - LAST
     rep, dp = lax.axis_index("rep"), lax.axis_index("dp")
     partner = 2 * (dp // 2) + 1 - dp % 2
     peer = (dp + 2) % 4
@@ -35,11 +41,11 @@
 
     def load_a(n, i):
         return pltpu.make_async_copy(
-            a.at[0, n, :, rows(order[i])], abuf.at[n % 2, :, rows(order[i])], asem.at[n % 2, i])
+            a.at[0, n, :, rows(order[i])], abuf.at[:, rows(order[i])], asem.at[i])
 
     def load_half(i, h):
         part = rows(order[i], h * 128, 128)
-        return pltpu.make_async_copy(a.at[0, 0, :, part], abuf.at[0, :, part], hsem.at[i // 2, h])
+        return pltpu.make_async_copy(a.at[0, 0, :, part], abuf.at[:, part], hsem.at[i // 2, h])
 
     def load_g(k):
         return pltpu.make_async_copy(g.at[0, k // per, :, columns(k)], gbuf.at[k % 3], gsem.at[k % 3])
@@ -75,6 +81,9 @@
     def cross(k):
         return remote(place(k, dp), place(k, dp), s4.at[k], r4.at[k], peer)
 
+    def cross_last():
+        return remote(place(inside - 1, dp), got, s4.at[inside - 1], r4.at[inside - 1], peer)
+
     def forward(k):
         return remote(place(k, peer), place(k, peer), s5.at[k], r5.at[k], partner)
 
@@ -82,7 +91,7 @@
         return lax.dot_general(left, right, (((0,), (0,)), ((), ())), preferred_element_type=jnp.float32)
 
     def product(k, i):
-        return dot(abuf[(k // per) % 2, :, rows(order[i])], gbuf[k % 3])
+        return dot(abuf[:, rows(order[i])], gbuf[k % 3])
 
     def both(here, there):
         return here + there.astype(jnp.float32)
@@ -90,7 +99,7 @@
     def first_part():
         def piece(j, i):
             r, h, c, w = PIECES[j]
-            return dot(abuf[0, :, rows(order[i], r, h)], gbuf[0, :, c:c + w])
+            return dot(abuf[:, rows(order[i], r, h)], gbuf[0, :, c:c + w])
 
         def send(j):
             r, h, c, w = PIECES[j]
@@ -119,8 +128,12 @@
                 load_a(0, 3).start()
         send(len(PIECES) - 1)
         load_g(2).start()
-        for i in range(4):
-            load_a(1, i).start()
+
+    def next_a(k, i):
+        @pl.when((k % per == per - 1) & (k + 1 < chunks))
+        def _():
+            load_a(k // per + 1, i).start()
+            load_a(k // per + 1, i + 2).start()
 
     def reduce_part(k):
         first = k % per == 0
@@ -143,6 +156,7 @@
         sb1[k % 2, 0] = product(k, 0).astype(jnp.bfloat16)
         term(k, 0).start()
         total[...] = product(k, 2)
+        next_a(k, 0)
         term(k, 0).wait_recv()
 
         @pl.when(k == 2)
@@ -175,11 +189,7 @@
         def _():
             load_g(k + 3).start()
 
-        @pl.when((k % per == per - 1) & (k // per + 2 < mats))
-        def _():
-            for i in range(4):
-                load_a(k // per + 2, i).start()
-
+        next_a(k, 1)
         term(k, 1).wait_recv()
 
         @pl.when(k == 0)
@@ -192,7 +202,11 @@
             half(k).wait_recv()
 
         out[k, rows(dp)] = both(both(total[...], rv1[k % 2, 1]), rv2[k % RING]).astype(jnp.bfloat16)
-        cross(k).start()
+
+        @pl.when(k < inside - 1)
+        def _():
+            cross(k).start()
+
         give(k).start()
 
     load_half(0, 0).start()
@@ -212,28 +226,38 @@
         def _():
             reduce_part(k + 1)
 
-        @pl.when(k < chunks)
-        def _():
-            owner_part(k)
-
-        @pl.when(k >= 2)
+        @pl.when(k == inside)
+        def _():
+            cross_last().start()
+
+        owner_part(k)
+
+        @pl.when((k >= 2) & (k < inside + 1))
         def _():
             cross(k - 2).wait_recv()
             forward(k - 2).start()
 
-    lax.fori_loop(0, chunks + 2, step, None)
+    lax.fori_loop(0, chunks, step, None)
+    tail = lb.shape[0]
+    la[:quarter] = out[chunks - 2, rows(dp)]
+    la[quarter:] = out[chunks - 1, rows(dp, 0, quarter - tail)]
+    lb[...] = out[chunks - 1, rows(dp, quarter - tail, tail)]
 
     for k in range(chunks - 2, chunks):
         for i in range(2):
             term(k, i).wait_send()
         half(k).wait_send()
 
+    for k in range(inside - 1, chunks):
+        give(k).wait()
+
     def drain(k, _):
         cross(k).wait_send()
         give(k).wait()
         forward(k).wait()
 
-    lax.fori_loop(0, chunks, drain, None)
+    lax.fori_loop(0, inside - 1, drain, None)
+    cross_last().wait()
 
 
 def write(done, out, sem):
@@ -247,6 +271,27 @@
         copy(k).start()
     for k in range(chunks):
         copy(k).wait()
+
+
+def patch(spots, *refs):
+    parts, out, sem = refs[:-3], refs[-2], refs[-1]
+    _, dim, wide = out.shape
+    per = wide // WIDTH
+    dp = lax.axis_index("dp")
+    copies = []
+    for i, pieces in enumerate(spots):
+        start = 0
+        for k, row, size in pieces:
+            for j, q in enumerate(((dp + 2) % 4, 3 - dp)):
+                rows = pl.ds(pl.multiple_of(q * (dim // 4) + row, 128), size)
+                copies.append(pltpu.make_async_copy(
+                    parts[2 * i + j].at[pl.ds(start, size)],
+                    out.at[k // per, rows, pl.ds((k % per) * WIDTH, WIDTH)], sem.at[len(copies)]))
+            start += size
+    for copy in copies:
+        copy.start()
+    for copy in copies:
+        copy.wait()
 
 
 def solution(mesh):
@@ -258,20 +303,22 @@
         dma = pltpu.SemaphoreType.DMA
         bf16, f32 = jnp.bfloat16, jnp.float32
         pieces = len(PIECES)
-        done = pl.pallas_call(
+        quarter = dim // 4
+        done, got, la, lb = pl.pallas_call(
             kernel,
-            out_shape=pltpu.VMEM((chunks, dim, WIDTH), bf16),
+            out_shape=tuple(pltpu.VMEM(shape, bf16) for shape in (
+                (chunks, dim, WIDTH), block, (2 * quarter - TAIL, WIDTH), (TAIL, WIDTH))),
             in_specs=[pl.BlockSpec(memory_space=pl.ANY)] * 2,
-            out_specs=pl.BlockSpec(memory_space=pltpu.VMEM),
+            out_specs=(pl.BlockSpec(memory_space=pltpu.VMEM),) * 4,
             scratch_shapes=[
-                pltpu.VMEM((2, tokens, dim), bf16),
+                pltpu.VMEM((tokens, dim), bf16),
                 pltpu.VMEM((3, tokens, WIDTH), bf16),
                 pltpu.VMEM((2, 2, *block), bf16),
                 pltpu.VMEM((2, 2, *block), bf16),
                 pltpu.VMEM(block, f32),
                 pltpu.VMEM((2, *block), bf16),
                 pltpu.VMEM((RING, *block), bf16),
-                dma((2, 4)), dma((2, 2)), dma((3,)), dma((2,)),
+                dma((4,)), dma((2, 2)), dma((3,)), dma((2,)),
                 dma((2, 2)), dma((chunks, 2)), dma((pieces,)), dma((pieces,)),
                 dma((2,)), dma((chunks,)), dma((pieces,)), dma((pieces,)),
                 dma((chunks,)), dma((chunks,)),
@@ -279,10 +326,31 @@
                 dma((chunks,)), dma((chunks,)),
             ],
             compiler_params=pltpu.CompilerParams(
-                collective_id=0, has_side_effects=True, vmem_limit_bytes=40_700_000),
+                collective_id=0, has_side_effects=True, vmem_limit_bytes=38_000_000),
             name="reduce",
         )(a, g)
-        return pl.pallas_call(
+
+        def across(x):
+            return lax.ppermute(x, "dp", [(d, (d + 2) % 4) for d in range(4)])
+
+        def beside(x):
+            return lax.ppermute(x, "dp", [(d, d ^ 1) for d in range(4)])
+
+        def patched(out, spots, *parts):
+            return pl.pallas_call(
+                functools.partial(patch, spots),
+                out_shape=jax.ShapeDtypeStruct(out.shape, out.dtype),
+                in_specs=[pl.BlockSpec(memory_space=pltpu.VMEM)] * len(parts) + [pl.BlockSpec(memory_space=pl.ANY)],
+                out_specs=pl.BlockSpec(memory_space=pl.ANY),
+                input_output_aliases={len(parts): 0},
+                scratch_shapes=[dma((2 * sum(len(s) for s in spots),))],
+                compiler_params=pltpu.CompilerParams(vmem_limit_bytes=1_000_000),
+            )(*parts, out)
+
+        near_a = across(la)
+        near_b = across(lb)
+        got_far = beside(got)
+        out = pl.pallas_call(
             write,
             out_shape=jax.ShapeDtypeStruct((mats, dim, wide), bf16),
             in_specs=[pl.BlockSpec(memory_space=pltpu.VMEM)],
@@ -291,6 +359,13 @@
             compiler_params=pltpu.CompilerParams(vmem_limit_bytes=1_000_000),
             name="write",
         )(done)
+        far_a = beside(near_a)
+        far_b = beside(near_b)
+        end = chunks - 1
+        out = patched(
+            out, (((end - 2, 0, quarter),), ((end - 1, 0, quarter), (end, 0, quarter - TAIL))),
+            got, got_far, near_a, far_a)
+        return patched(out, (((end, quarter - TAIL, TAIL),),), near_b, far_b)
 
     both = P(("rep", "dp"))
     return jax.shard_map(step, mesh=mesh, in_specs=(both, both), out_specs=P("rep"), check_vma=False)

time: 304 us -> 308 us (1.013)
  waiting for transfers between devices: 0 us -> 18.5 us
  Pallas kernels: 304 us -> 289 us
    ppermute x0 -> x5, waiting for transfers between devices: none -> 18.5 us  [the longest x2 18.5 us: across(): return lax.ppermute(x, 'dp', [(d, (d + 2) % 4) for d in range(4)])]
    pallas_call x1 -> x3, Pallas kernels: 295 us -> 280 us  [the longest x1 278 us: step(): pl.pallas_call(kernel, out_shape=tuple((pltpu.VMEM(shape, bf16) for shape...]
  transfers between devices with their start and end apart: 0 -> 5, of which waited for: 0 -> 2; matrix products, arithmetic and copies ran while one was open for 0% -> 0% of each run, Pallas kernels for 0% -> 3%
where the time goes in v3:
time: 308 us
  Pallas kernels  289 us (94%)
  waiting for transfers between devices  18.5 us (6%)
    pallas_call x1, Pallas kernels, step(): pl.pallas_call(kernel, out_shape=tuple((pltpu.VMEM(shape, bf16) for shape...  278 us
    ppermute x2, waiting for transfers between devices, across(): return lax.ppermute(x, 'dp', [(d, (d + 2) % 4) for d in range(4)])  18.5 us
    pallas_call x1, Pallas kernels, step(): pl.pallas_call(write, out_shape=jax.ShapeDtypeStruct((mats, dim, wide), b...  8.86 us
  transfers between devices with their start and end apart: 5, of which 2 were waited for; matrix products, arithmetic and copies ran while one was open for 0% of the time, Pallas kernels for 3%

profile of v3, /device:TPU:0, one launch (start us, length us, event | category | flops | bytes accessed | tf_op | source)
XLA Modules:
  0.0 308.3 jit_solution(4752758580328491142)
XLA Ops:
  0.0 277.7 %reduce.1 = (bf16[20,1024,640]{2,1,0:T(8,128)(2,1)S(1)}, bf16[256,640]{1,0:T(8,128)(2,1)S(1)}, bf16[384,640]{1,0:T(8,128)(2,1)S(1)}, bf16[128,640]{1,0:T(8,128)(2,1)S(1)}) custom-call(bf16[1,4,4096,1024]{3,2,1,0:T(8,128)(2,1)} %a.1, bf16[1,4,4096,3200]{3,2,1,0:T(8,128)(2,1)} %g.1), custom_call_target="tpu_custom_call" | custom-call | tf_op jit(solution)/shard_map/reduce/pallas_call | solution.py:307
  277.7 0.2 collective-permute-start.3
  277.9 12.7 %collective-permute-done.3.refs_2_ = bf16[384,640]{1,0:T(8,128)(2,1)S(1)} collective-permute-done((bf16[384,640]{1,0:T(8,128)(2,1)S(1)}, bf16[384,640]{1,0:T(8,128)(2,1)S(1)}, u32[]{:S(2)}, u32[]{:S(2)}) %collective-permute-start.3) | collective-permute-done | bytes 491552 | tf_op jit(solution)/shard_map/ppermute | solution.py:334
  290.6 0.0 collective-permute-start.4
  290.6 0.5 collective-permute-start.2
  291.2 0.3 collective-permute-start
  291.4 5.8 %collective-permute-done.refs_0_ = bf16[128,640]{1,0:T(8,128)(2,1)S(1)} collective-permute-done((bf16[128,640]{1,0:T(8,128)(2,1)S(1)}, bf16[128,640]{1,0:T(8,128)(2,1)S(1)}, u32[]{:S(2)}, u32[]{:S(2)}) %collective-permute-start) | collective-permute-done | bytes 163872 | tf_op jit(solution)/shard_map/ppermute | solution.py:334
  297.3 0.0 collective-permute-start.1
  297.3 8.9 %write.1.refs_4_ = bf16[4,1024,3200]{2,1,0:T(8,128)(2,1)} custom-call(bf16[20,1024,640]{2,1,0:T(8,128)(2,1)S(1)} %get-tuple-element.12.done), custom_call_target="tpu_custom_call" | custom-call | tf_op jit(solution)/shard_map/write/pallas_call | solution.py:353
  306.1 0.0 collective-permute-done.2.refs_1_
  306.1 0.0 collective-permute-done.4.refs_3_
  306.2 1.2 shard_map.28.refs_2_
  307.4 0.0 collective-permute-done.1.refs_1_
  307.4 0.8 shard_map.29
Async XLA Ops:
  277.7 12.9 %collective-permute-start.3 = (bf16[384,640]{1,0:T(8,128)(2,1)S(1)}, bf16[384,640]{1,0:T(8,128)(2,1)S(1)}, u32[]{:S(2)}, u32[]{:S(2)}) collective-permute-start(bf16[384,640]{1,0:T(8,128)(2,1)S(1)} %get-tuple-element.11), channel_id=1, source_target_pairs={{0,2},{1,3},{2,0},{3,1},{4,6},{5,7},{6,4},{7,5}} | collective-permute-start | bytes 1474568 | tf_op jit(solution)/shard_map/ppermute | solution.py:334
  290.6 15.5 %collective-permute-start.4 = (bf16[384,640]{1,0:T(8,128)(2,1)S(1)}, bf16[384,640]{1,0:T(8,128)(2,1)S(1)}, u32[]{:S(2)}, u32[]{:S(2)}) collective-permute-start(bf16[384,640]{1,0:T(8,128)(2,1)S(1)} %collective-permute-done.3.refs_2_), channel_id=1, source_target_pairs={{0,1},{1,0},{2,3},{3,2},{4,5},{5,4},{6,7},{7,6}} | collective-permute-start | bytes 1474568 | tf_op jit(solution)/shard_map/ppermute | solution.py:337
  290.6 15.5 %collective-permute-start.2 = (bf16[256,640]{1,0:T(8,128)(2,1)S(1)}, bf16[256,640]{1,0:T(8,128)(2,1)S(1)}, u32[]{:S(2)}, u32[]{:S(2)}) collective-permute-start(bf16[256,640]{1,0:T(8,128)(2,1)S(1)} %get-tuple-element.10.refs_0_), channel_id=1, source_target_pairs={{0,1},{1,0},{2,3},{3,2},{4,5},{5,4},{6,7},{7,6}} | collective-permute-start | bytes 983048 | tf_op jit(solution)/shard_map/ppermute | solution.py:337
  291.2 6.1 %collective-permute-start = (bf16[128,640]{1,0:T(8,128)(2,1)S(1)}, bf16[128,640]{1,0:T(8,128)(2,1)S(1)}, u32[]{:S(2)}, u32[]{:S(2)}) collective-permute-start(bf16[128,640]{1,0:T(8,128)(2,1)S(1)} %get-tuple-element.9), channel_id=1, source_target_pairs={{0,2},{1,3},{2,0},{3,1},{4,6},{5,7},{6,4},{7,5}} | collective-permute-start | bytes 491528 | tf_op jit(solution)/shard_map/ppermute | solution.py:334
  297.3 10.1 %collective-permute-start.1 = (bf16[128,640]{1,0:T(8,128)(2,1)S(1)}, bf16[128,640]{1,0:T(8,128)(2,1)S(1)}, u32[]{:S(2)}, u32[]{:S(2)}) collective-permute-start(bf16[128,640]{1,0:T(8,128)(2,1)S(1)} %collective-permute-done.refs_0_), channel_id=1, source_target_pairs={{0,1},{1,0},{2,3},{3,2},{4,5},{5,4},{6,7},{7,6}} | collective-permute-start | bytes 491528 | tf_op jit(solution)/shard_map/ppermute | solution.py:337

commit v4 on v3

--- a/solution.py
+++ b/solution.py
@@ -11,14 +11,15 @@
 MESH = pl.DeviceIdType.MESH
 WIDTH = 640
 RING = 4
-PIECES = ((0, 128, 0, 256), (128, 128, 0, 256), (0, 256, 256, 384))
+SPLIT = 192
+PIECES = ((0, 0, 128, 0, 256), (0, 128, 128, 0, 256), (0, 0, 128, 256, 384), (0, 128, 128, 256, 384), (1, 0, 256, 0, 256), (1, 0, 256, 256, 384))
 LAST = 2
 TAIL = 128
 
 
 def kernel(
     a, g, out, got, la, lb, abuf, gbuf, sb1, rv1, total, sb2, rv2,
-    asem, hsem, gsem, g0sem, s1, r1, p1, q1, s2, r2, p2, q2, s3, r3, s4, r4, s5, r5,
+    asem, hsem, gsem, g0sem, s1, r1, p1, q1, s2, r2, p2, q2, s3, r3, s4, r4, s5, r5, s6, r6, turn,
 ):
     _, mats, _, dim = a.shape
     quarter = dim // 4
@@ -63,17 +64,17 @@
         return remote(sb1.at[k % 2, i], rv1.at[k % 2, i], s1.at[k % 2, i], r1.at[k, i], partner)
 
     def term_piece(j):
-        r, h, c, w = PIECES[j]
+        k, r, h, c, w = PIECES[j]
         part = (pl.ds(r, h), pl.ds(c, w))
-        return remote(sb1.at[0, 0, *part], rv1.at[0, 0, *part], p1.at[j], q1.at[j], partner)
+        return remote(sb1.at[k, 0, *part], rv1.at[k, 0, *part], p1.at[j], q1.at[j], partner)
 
     def half(k):
         return remote(sb2.at[k % 2], rv2.at[k % RING], s2.at[k % 2], r2.at[k], peer)
 
     def half_piece(j):
-        r, h, c, w = PIECES[j]
+        k, r, h, c, w = PIECES[j]
         part = (pl.ds(r, h), pl.ds(c, w))
-        return remote(sb2.at[0, *part], rv2.at[0, *part], p2.at[j], q2.at[j], peer)
+        return remote(sb2.at[k, *part], rv2.at[k, *part], p2.at[j], q2.at[j], peer)
 
     def give(k):
         return remote(place(k, dp), place(k, dp), s3.at[k], r3.at[k], partner)
@@ -81,8 +82,10 @@
     def cross(k):
         return remote(place(k, dp), place(k, dp), s4.at[k], r4.at[k], peer)
 
-    def cross_last():
-        return remote(place(inside - 1, dp), got, s4.at[inside - 1], r4.at[inside - 1], peer)
+    def cross_last(j):
+        start, size = ((0, SPLIT), (SPLIT, quarter - SPLIT))[j]
+        return remote(out.at[inside - 1, pl.ds(pl.multiple_of(dp * quarter + start, 16), size)],
+                      got.at[pl.ds(start, size)], s6.at[j], r6.at[j], peer)
 
     def forward(k):
         return remote(place(k, peer), place(k, peer), s5.at[k], r5.at[k], partner)
@@ -98,29 +101,40 @@
 
     def first_part():
         def piece(j, i):
-            r, h, c, w = PIECES[j]
-            return dot(abuf[:, rows(order[i], r, h)], gbuf[0, :, c:c + w])
+            k, r, h, c, w = PIECES[j]
+            return dot(abuf[:, rows(order[i], r, h)], gbuf[k, :, c:c + w])
 
         def send(j):
-            r, h, c, w = PIECES[j]
+            k, r, h, c, w = PIECES[j]
             term_piece(j).wait_recv()
-            sb2[0, r:r + h, c:c + w] = both(total[r:r + h, c:c + w], rv1[0, 0, r:r + h, c:c + w]).astype(jnp.bfloat16)
+            sb2[k, r:r + h, c:c + w] = both(total[r:r + h, c:c + w], rv1[k, 0, r:r + h, c:c + w]).astype(jnp.bfloat16)
             half_piece(j).start()
 
-        for j, (r, h, c, w) in enumerate(PIECES):
+        waited = set()
+
+        def need(name, load, *args):
+            if name not in waited:
+                waited.add(name)
+                load(*args).wait()
+
+        for j, (k, r, h, c, w) in enumerate(PIECES):
+            halves = [x for x in range(2) if k == 0 and r < (x + 1) * 128 and r + h > x * 128]
+            for x in halves:
+                need((0, x), load_half, 0, x)
+            if k == 0 and c < 256:
+                need("g", load_g0, 0, 0, 256)
+            if k == 0 and c + w > 256:
+                need("h", load_g0, 1, 256, 384)
+            if k == 1:
+                need("k", load_g, 1)
+            sb1[k, 0, r:r + h, c:c + w] = piece(j, 0).astype(jnp.bfloat16)
             if j == 0:
-                load_half(0, 0).wait()
-                load_g0(0, 0, 256).wait()
-            if j == 1:
-                load_half(0, 1).wait()
-            if j == 2:
-                load_g0(1, 256, 384).wait()
-            sb1[0, 0, r:r + h, c:c + w] = piece(j, 0).astype(jnp.bfloat16)
+                pl.semaphore_wait(pltpu.get_barrier_semaphore(), 2)
             term_piece(j).start()
             if j:
                 send(j - 1)
-            if j < 2:
-                load_half(2, j).wait()
+            for x in halves:
+                need((2, x), load_half, 2, x)
             total[r:r + h, c:c + w] = piece(j, 2)
             if j == 0:
                 load_g(1).start()
@@ -129,6 +143,11 @@
         send(len(PIECES) - 1)
         load_g(2).start()
 
+    def pieces_of(k, act):
+        for j in range(len(PIECES)):
+            if PIECES[j][0] == k:
+                act(j)
+
     def next_a(k, i):
         @pl.when((k % per == per - 1) & (k + 1 < chunks))
         def _():
@@ -144,12 +163,13 @@
             load_a(k // per, 0).wait()
             load_a(k // per, 2).wait()
 
-        @pl.when(k == 2)
-        def _():
-            for j in range(len(PIECES)):
-                term_piece(j).wait_send()
-
-        @pl.when(k > 2)
+        for early in range(2):
+            @pl.when(k == early + 2)
+            def _():
+                pieces_of(early, lambda j: term_piece(j).wait_send())
+                pieces_of(early, lambda j: half_piece(j).wait_send())
+
+        @pl.when(k > 3)
         def _():
             term(k - 2, 0).wait_send()
 
@@ -159,12 +179,7 @@
         next_a(k, 0)
         term(k, 0).wait_recv()
 
-        @pl.when(k == 2)
-        def _():
-            for j in range(len(PIECES)):
-                half_piece(j).wait_send()
-
-        @pl.when(k > 2)
+        @pl.when(k > 3)
         def _():
             half(k - 2).wait_send()
 
@@ -192,12 +207,12 @@
         next_a(k, 1)
         term(k, 1).wait_recv()
 
-        @pl.when(k == 0)
-        def _():
-            for j in range(len(PIECES)):
-                half_piece(j).wait_recv()
-
-        @pl.when(k > 0)
+        for early in range(2):
+            @pl.when(k == early)
+            def _():
+                pieces_of(early, lambda j: half_piece(j).wait_recv())
+
+        @pl.when(k > 1)
         def _():
             half(k).wait_recv()
 
@@ -218,17 +233,17 @@
     barrier = pltpu.get_barrier_semaphore()
     for other in (partner, peer):
         pl.semaphore_signal(barrier, inc=1, device_id=(rep, other), device_id_type=MESH)
-    pl.semaphore_wait(barrier, 2)
     first_part()
 
     def step(k, _):
-        @pl.when(k + 1 < chunks)
+        @pl.when((k > 0) & (k + 1 < chunks))
         def _():
             reduce_part(k + 1)
 
-        @pl.when(k == inside)
-        def _():
-            cross_last().start()
+        @pl.when((k == inside) & (dp % 2 == 0))
+        def _():
+            cross_last(0).start()
+            cross_last(1).start()
 
         owner_part(k)
 
@@ -238,6 +253,19 @@
             forward(k - 2).start()
 
     lax.fori_loop(0, chunks, step, None)
+
+    @pl.when(dp % 2 == 0)
+    def _():
+        cross_last(0).wait_send()
+        pl.semaphore_signal(turn, inc=1, device_id=(rep, partner), device_id_type=MESH)
+
+    @pl.when(dp % 2 == 1)
+    def _():
+        pl.semaphore_wait(turn, 1)
+        cross_last(0).start()
+        cross_last(1).start()
+        cross_last(0).wait_send()
+
     tail = lb.shape[0]
     la[:quarter] = out[chunks - 2, rows(dp)]
     la[quarter:] = out[chunks - 1, rows(dp, 0, quarter - tail)]
@@ -257,7 +285,8 @@
         forward(k).wait()
 
     lax.fori_loop(0, inside - 1, drain, None)
-    cross_last().wait()
+    cross_last(0).wait_recv()
+    cross_last(1).wait()
 
 
 def write(done, out, sem):
@@ -323,7 +352,7 @@
                 dma((2,)), dma((chunks,)), dma((pieces,)), dma((pieces,)),
                 dma((chunks,)), dma((chunks,)),
                 dma((chunks,)), dma((chunks,)),
-                dma((chunks,)), dma((chunks,)),
+                dma((chunks,)), dma((chunks,)), dma((2,)), dma((2,)), pltpu.SemaphoreType.REGULAR,
             ],
             compiler_params=pltpu.CompilerParams(
                 collective_id=0, has_side_effects=True, vmem_limit_bytes=38_000_000),

time: 308 us -> 306 us (level)
  Pallas kernels: 289 us -> 285 us
    pallas_call x1, Pallas kernels: 278 us -> 274 us  [step(): pl.pallas_call(kernel, out_shape=tuple((pltpu.VMEM(shape, bf16) for shape...]
where the time goes in v4:
time: 306 us
  Pallas kernels  285 us (93%)
  waiting for transfers between devices  18.3 us (6%)
    pallas_call x1, Pallas kernels, step(): pl.pallas_call(kernel, out_shape=tuple((pltpu.VMEM(shape, bf16) for shape...  274 us
    ppermute x2, waiting for transfers between devices, across(): return lax.ppermute(x, 'dp', [(d, (d + 2) % 4) for d in range(4)])  18.3 us
    pallas_call x1, Pallas kernels, step(): pl.pallas_call(write, out_shape=jax.ShapeDtypeStruct((mats, dim, wide), b...  8.86 us
  transfers between devices with their start and end apart: 5, of which 2 were waited for; matrix products, arithmetic and copies ran while one was open for 0% of the time, Pallas kernels for 3%

profile of v4, /device:TPU:0, one launch (start us, length us, event | category | flops | bytes accessed | tf_op | source)
XLA Modules:
  0.0 305.6 jit_solution(6065946538124865478)
XLA Ops:
  0.0 274.0 %reduce.1 = (bf16[20,1024,640]{2,1,0:T(8,128)(2,1)S(1)}, bf16[256,640]{1,0:T(8,128)(2,1)S(1)}, bf16[384,640]{1,0:T(8,128)(2,1)S(1)}, bf16[128,640]{1,0:T(8,128)(2,1)S(1)}) custom-call(bf16[1,4,4096,1024]{3,2,1,0:T(8,128)(2,1)} %a.1, bf16[1,4,4096,3200]{3,2,1,0:T(8,128)(2,1)} %g.1), custom_call_target="tpu_custom_call" | custom-call | tf_op jit(solution)/shard_map/reduce/pallas_call | solution.py:336
  274.0 0.0 collective-permute-start.3
  274.1 11.7 %collective-permute-done.3.refs_2_ = bf16[384,640]{1,0:T(8,128)(2,1)S(1)} collective-permute-done((bf16[384,640]{1,0:T(8,128)(2,1)S(1)}, bf16[384,640]{1,0:T(8,128)(2,1)S(1)}, u32[]{:S(2)}, u32[]{:S(2)}) %collective-permute-start.3) | collective-permute-done | bytes 491552 | tf_op jit(solution)/shard_map/ppermute | solution.py:363
  285.8 2.2 collective-permute-start.4
  288.0 0.0 collective-permute-start.2
  288.0 0.0 collective-permute-start
  288.0 6.6 %collective-permute-done.refs_0_ = bf16[128,640]{1,0:T(8,128)(2,1)S(1)} collective-permute-done((bf16[128,640]{1,0:T(8,128)(2,1)S(1)}, bf16[128,640]{1,0:T(8,128)(2,1)S(1)}, u32[]{:S(2)}, u32[]{:S(2)}) %collective-permute-start) | collective-permute-done | bytes 163872 | tf_op jit(solution)/shard_map/ppermute | solution.py:363
  294.6 0.0 collective-permute-start.1
  294.6 8.9 %write.1.refs_4_ = bf16[4,1024,3200]{2,1,0:T(8,128)(2,1)} custom-call(bf16[20,1024,640]{2,1,0:T(8,128)(2,1)S(1)} %get-tuple-element.12.done), custom_call_target="tpu_custom_call" | custom-call | tf_op jit(solution)/shard_map/write/pallas_call | solution.py:382
  303.5 0.0 collective-permute-done.2.refs_1_
  303.5 0.0 collective-permute-done.4.refs_3_
  303.5 1.2 shard_map.28.refs_2_
  304.7 0.0 collective-permute-done.1.refs_1_
  304.7 0.8 shard_map.29
Async XLA Ops:
  274.0 11.7 %collective-permute-start.3 = (bf16[384,640]{1,0:T(8,128)(2,1)S(1)}, bf16[384,640]{1,0:T(8,128)(2,1)S(1)}, u32[]{:S(2)}, u32[]{:S(2)}) collective-permute-start(bf16[384,640]{1,0:T(8,128)(2,1)S(1)} %get-tuple-element.11), channel_id=1, source_target_pairs={{0,2},{1,3},{2,0},{3,1},{4,6},{5,7},{6,4},{7,5}} | collective-permute-start | bytes 1474568 | tf_op jit(solution)/shard_map/ppermute | solution.py:363
  285.8 17.7 %collective-permute-start.4 = (bf16[384,640]{1,0:T(8,128)(2,1)S(1)}, bf16[384,640]{1,0:T(8,128)(2,1)S(1)}, u32[]{:S(2)}, u32[]{:S(2)}) collective-permute-start(bf16[384,640]{1,0:T(8,128)(2,1)S(1)} %collective-permute-done.3.refs_2_), channel_id=1, source_target_pairs={{0,1},{1,0},{2,3},{3,2},{4,5},{5,4},{6,7},{7,6}} | collective-permute-start | bytes 1474568 | tf_op jit(solution)/shard_map/ppermute | solution.py:366
  288.0 15.5 %collective-permute-start.2 = (bf16[256,640]{1,0:T(8,128)(2,1)S(1)}, bf16[256,640]{1,0:T(8,128)(2,1)S(1)}, u32[]{:S(2)}, u32[]{:S(2)}) collective-permute-start(bf16[256,640]{1,0:T(8,128)(2,1)S(1)} %get-tuple-element.10.refs_0_), channel_id=1, source_target_pairs={{0,1},{1,0},{2,3},{3,2},{4,5},{5,4},{6,7},{7,6}} | collective-permute-start | bytes 983048 | tf_op jit(solution)/shard_map/ppermute | solution.py:366
  288.0 6.6 %collective-permute-start = (bf16[128,640]{1,0:T(8,128)(2,1)S(1)}, bf16[128,640]{1,0:T(8,128)(2,1)S(1)}, u32[]{:S(2)}, u32[]{:S(2)}) collective-permute-start(bf16[128,640]{1,0:T(8,128)(2,1)S(1)} %get-tuple-element.9), channel_id=1, source_target_pairs={{0,2},{1,3},{2,0},{3,1},{4,6},{5,7},{6,4},{7,5}} | collective-permute-start | bytes 491528 | tf_op jit(solution)/shard_map/ppermute | solution.py:363
  294.6 10.1 %collective-permute-start.1 = (bf16[128,640]{1,0:T(8,128)(2,1)S(1)}, bf16[128,640]{1,0:T(8,128)(2,1)S(1)}, u32[]{:S(2)}, u32[]{:S(2)}) collective-permute-start(bf16[128,640]{1,0:T(8,128)(2,1)S(1)} %collective-permute-done.refs_0_), channel_id=1, source_target_pairs={{0,1},{1,0},{2,3},{3,2},{4,5},{5,4},{6,7},{7,6}} | collective-permute-start | bytes 491528 | tf_op jit(solution)/shard_map/ppermute | solution.py:366

commit v5 on v4

--- a/solution.py
+++ b/solution.py
@@ -19,7 +19,7 @@
 
 def kernel(
     a, g, out, got, la, lb, abuf, gbuf, sb1, rv1, total, sb2, rv2,
-    asem, hsem, gsem, g0sem, s1, r1, p1, q1, s2, r2, p2, q2, s3, r3, s4, r4, s5, r5, s6, r6, turn,
+    asem, hsem, gsem, g0sem, s1, r1, q1, s2, r2, s3, r3, s4, r4, s5, r5, s6, r6, turn,
 ):
     _, mats, _, dim = a.shape
     quarter = dim // 4
@@ -61,26 +61,26 @@
             device_id=(rep, to), device_id_type=MESH)
 
     def term(k, i):
-        return remote(sb1.at[k % 2, i], rv1.at[k % 2, i], s1.at[k % 2, i], r1.at[k, i], partner)
+        return remote(sb1.at[k % 2, i], rv1.at[k % 2, i], s1.at[k % 2, i], r1.at[k % 2, i], partner)
 
     def term_piece(j):
         k, r, h, c, w = PIECES[j]
         part = (pl.ds(r, h), pl.ds(c, w))
-        return remote(sb1.at[k, 0, *part], rv1.at[k, 0, *part], p1.at[j], q1.at[j], partner)
+        return remote(sb1.at[k, 0, *part], rv1.at[k, 0, *part], s1.at[k, 0], q1.at[j % 4], partner)
 
     def half(k):
-        return remote(sb2.at[k % 2], rv2.at[k % RING], s2.at[k % 2], r2.at[k], peer)
+        return remote(sb2.at[k % 2], rv2.at[k % RING], s2.at[k % 2], r2.at[k % RING], peer)
 
     def half_piece(j):
         k, r, h, c, w = PIECES[j]
         part = (pl.ds(r, h), pl.ds(c, w))
-        return remote(sb2.at[k, *part], rv2.at[k, *part], p2.at[j], q2.at[j], peer)
+        return remote(sb2.at[k, *part], rv2.at[k, *part], s2.at[k], r2.at[k], peer)
 
     def give(k):
-        return remote(place(k, dp), place(k, dp), s3.at[k], r3.at[k], partner)
+        return remote(place(k, dp), place(k, dp), s3.at[k % RING], r3.at[k % RING], partner)
 
     def cross(k):
-        return remote(place(k, dp), place(k, dp), s4.at[k], r4.at[k], peer)
+        return remote(place(k, dp), place(k, dp), s4.at[k % RING], r4.at[k % RING], peer)
 
     def cross_last(j):
         start, size = ((0, SPLIT), (SPLIT, quarter - SPLIT))[j]
@@ -88,7 +88,7 @@
                       got.at[pl.ds(start, size)], s6.at[j], r6.at[j], peer)
 
     def forward(k):
-        return remote(place(k, peer), place(k, peer), s5.at[k], r5.at[k], partner)
+        return remote(place(k, peer), place(k, peer), s5.at[k % RING], r5.at[k % RING], partner)
 
     def dot(left, right):
         return lax.dot_general(left, right, (((0,), (0,)), ((), ())), preferred_element_type=jnp.float32)
@@ -143,11 +143,6 @@
         send(len(PIECES) - 1)
         load_g(2).start()
 
-    def pieces_of(k, act):
-        for j in range(len(PIECES)):
-            if PIECES[j][0] == k:
-                act(j)
-
     def next_a(k, i):
         @pl.when((k % per == per - 1) & (k + 1 < chunks))
         def _():
@@ -163,15 +158,7 @@
             load_a(k // per, 0).wait()
             load_a(k // per, 2).wait()
 
-        for early in range(2):
-            @pl.when(k == early + 2)
-            def _():
-                pieces_of(early, lambda j: term_piece(j).wait_send())
-                pieces_of(early, lambda j: half_piece(j).wait_send())
-
-        @pl.when(k > 3)
-        def _():
-            term(k - 2, 0).wait_send()
+        term(k - 2, 0).wait_send()
 
         sb1[k % 2, 0] = product(k, 0).astype(jnp.bfloat16)
         term(k, 0).start()
@@ -179,9 +166,7 @@
         next_a(k, 0)
         term(k, 0).wait_recv()
 
-        @pl.when(k > 3)
-        def _():
-            half(k - 2).wait_send()
+        half(k - 2).wait_send()
 
         sb2[k % 2] = both(total[...], rv1[k % 2, 0]).astype(jnp.bfloat16)
         half(k).start()
@@ -207,20 +192,21 @@
         next_a(k, 1)
         term(k, 1).wait_recv()
 
-        for early in range(2):
-            @pl.when(k == early)
-            def _():
-                pieces_of(early, lambda j: half_piece(j).wait_recv())
-
-        @pl.when(k > 1)
-        def _():
-            half(k).wait_recv()
+        half(k).wait_recv()
 
         out[k, rows(dp)] = both(both(total[...], rv1[k % 2, 1]), rv2[k % RING]).astype(jnp.bfloat16)
 
+        @pl.when((k >= RING) & (k < inside - 1))
+        def _():
+            cross(k - RING).wait_send()
+
         @pl.when(k < inside - 1)
         def _():
             cross(k).start()
+
+        @pl.when(k >= RING)
+        def _():
+            give(k - RING).wait_send()
 
         give(k).start()
 
@@ -250,7 +236,20 @@
         @pl.when((k >= 2) & (k < inside + 1))
         def _():
             cross(k - 2).wait_recv()
+
+            @pl.when(k >= RING + 2)
+            def _():
+                forward(k - RING - 2).wait_send()
+
             forward(k - 2).start()
+
+        @pl.when(k >= 2)
+        def _():
+            give(k - 2).wait_recv()
+
+        @pl.when(k >= 4)
+        def _():
+            forward(k - 4).wait_recv()
 
     lax.fori_loop(0, chunks, step, None)
 
@@ -276,15 +275,15 @@
             term(k, i).wait_send()
         half(k).wait_send()
 
-    for k in range(inside - 1, chunks):
-        give(k).wait()
-
-    def drain(k, _):
+    for k in range(chunks - RING, chunks):
+        give(k).wait_send()
+    for k in range(chunks - 2, chunks):
+        give(k).wait_recv()
+    for k in range(inside - 1 - RING, inside - 1):
         cross(k).wait_send()
-        give(k).wait()
-        forward(k).wait()
-
-    lax.fori_loop(0, inside - 1, drain, None)
+        forward(k).wait_send()
+    for k in range(chunks - 4, inside - 1):
+        forward(k).wait_recv()
     cross_last(0).wait_recv()
     cross_last(1).wait()
 
@@ -331,7 +330,6 @@
         block = (dim // 4, WIDTH)
         dma = pltpu.SemaphoreType.DMA
         bf16, f32 = jnp.bfloat16, jnp.float32
-        pieces = len(PIECES)
         quarter = dim // 4
         done, got, la, lb = pl.pallas_call(
             kernel,
@@ -348,11 +346,11 @@
                 pltpu.VMEM((2, *block), bf16),
                 pltpu.VMEM((RING, *block), bf16),
                 dma((4,)), dma((2, 2)), dma((3,)), dma((2,)),
-                dma((2, 2)), dma((chunks, 2)), dma((pieces,)), dma((pieces,)),
-                dma((2,)), dma((chunks,)), dma((pieces,)), dma((pieces,)),
-                dma((chunks,)), dma((chunks,)),
-                dma((chunks,)), dma((chunks,)),
-                dma((chunks,)), dma((chunks,)), dma((2,)), dma((2,)), pltpu.SemaphoreType.REGULAR,
+                dma((2, 2)), dma((2, 2)), dma((4,)),
+                dma((2,)), dma((RING,)),
+                dma((RING,)), dma((RING,)),
+                dma((RING,)), dma((RING,)),
+                dma((RING,)), dma((RING,)), dma((2,)), dma((2,)), pltpu.SemaphoreType.REGULAR,
             ],
             compiler_params=pltpu.CompilerParams(
                 collective_id=0, has_side_effects=True, vmem_limit_bytes=38_000_000),

time: 306 us -> 304 us (level)
  no operation moved by 1% of the time
where the time goes in v5:
time: 304 us
  Pallas kernels  283 us (93%)
  waiting for transfers between devices  18.3 us (6%)
    pallas_call x1, Pallas kernels, step(): pl.pallas_call(kernel, out_shape=tuple((pltpu.VMEM(shape, bf16) for shape...  273 us
    ppermute x2, waiting for transfers between devices, across(): return lax.ppermute(x, 'dp', [(d, (d + 2) % 4) for d in range(4)])  18.3 us
    pallas_call x1, Pallas kernels, step(): pl.pallas_call(write, out_shape=jax.ShapeDtypeStruct((mats, dim, wide), b...  8.86 us
  transfers between devices with their start and end apart: 5, of which 2 were waited for; matrix products, arithmetic and copies ran while one was open for 0% of the time, Pallas kernels for 3%

profile of v5, /device:TPU:0, one launch (start us, length us, event | category | flops | bytes accessed | tf_op | source)
XLA Modules:
  0.0 304.1 jit_solution(6642728282098950882)
XLA Ops:
  0.0 272.5 %reduce.1 = (bf16[20,1024,640]{2,1,0:T(8,128)(2,1)S(1)}, bf16[256,640]{1,0:T(8,128)(2,1)S(1)}, bf16[384,640]{1,0:T(8,128)(2,1)S(1)}, bf16[128,640]{1,0:T(8,128)(2,1)S(1)}) custom-call(bf16[1,4,4096,1024]{3,2,1,0:T(8,128)(2,1)} %a.1, bf16[1,4,4096,3200]{3,2,1,0:T(8,128)(2,1)} %g.1), custom_call_target="tpu_custom_call" | custom-call | tf_op jit(solution)/shard_map/reduce/pallas_call | solution.py:334
  272.5 0.0 collective-permute-start.3
  272.6 11.7 %collective-permute-done.3.refs_2_ = bf16[384,640]{1,0:T(8,128)(2,1)S(1)} collective-permute-done((bf16[384,640]{1,0:T(8,128)(2,1)S(1)}, bf16[384,640]{1,0:T(8,128)(2,1)S(1)}, u32[]{:S(2)}, u32[]{:S(2)}) %collective-permute-start.3) | collective-permute-done | bytes 491552 | tf_op jit(solution)/shard_map/ppermute | solution.py:361
  284.3 2.2 collective-permute-start.4
  286.5 0.0 collective-permute-start.2
  286.5 0.0 collective-permute-start
  286.5 6.6 %collective-permute-done.refs_0_ = bf16[128,640]{1,0:T(8,128)(2,1)S(1)} collective-permute-done((bf16[128,640]{1,0:T(8,128)(2,1)S(1)}, bf16[128,640]{1,0:T(8,128)(2,1)S(1)}, u32[]{:S(2)}, u32[]{:S(2)}) %collective-permute-start) | collective-permute-done | bytes 163872 | tf_op jit(solution)/shard_map/ppermute | solution.py:361
  293.1 0.0 collective-permute-start.1
  293.1 8.9 %write.1.refs_4_ = bf16[4,1024,3200]{2,1,0:T(8,128)(2,1)} custom-call(bf16[20,1024,640]{2,1,0:T(8,128)(2,1)S(1)} %get-tuple-element.12.done), custom_call_target="tpu_custom_call" | custom-call | tf_op jit(solution)/shard_map/write/pallas_call | solution.py:380
  302.0 0.0 collective-permute-done.2.refs_1_
  302.0 0.0 collective-permute-done.4.refs_3_
  302.0 1.2 shard_map.28.refs_2_
  303.2 0.0 collective-permute-done.1.refs_1_
  303.2 0.8 shard_map.29
Async XLA Ops:
  272.5 11.7 %collective-permute-start.3 = (bf16[384,640]{1,0:T(8,128)(2,1)S(1)}, bf16[384,640]{1,0:T(8,128)(2,1)S(1)}, u32[]{:S(2)}, u32[]{:S(2)}) collective-permute-start(bf16[384,640]{1,0:T(8,128)(2,1)S(1)} %get-tuple-element.11), channel_id=1, source_target_pairs={{0,2},{1,3},{2,0},{3,1},{4,6},{5,7},{6,4},{7,5}} | collective-permute-start | bytes 1474568 | tf_op jit(solution)/shard_map/ppermute | solution.py:361
  284.3 17.7 %collective-permute-start.4 = (bf16[384,640]{1,0:T(8,128)(2,1)S(1)}, bf16[384,640]{1,0:T(8,128)(2,1)S(1)}, u32[]{:S(2)}, u32[]{:S(2)}) collective-permute-start(bf16[384,640]{1,0:T(8,128)(2,1)S(1)} %collective-permute-done.3.refs_2_), channel_id=1, source_target_pairs={{0,1},{1,0},{2,3},{3,2},{4,5},{5,4},{6,7},{7,6}} | collective-permute-start | bytes 1474568 | tf_op jit(solution)/shard_map/ppermute | solution.py:364
  286.5 15.5 %collective-permute-start.2 = (bf16[256,640]{1,0:T(8,128)(2,1)S(1)}, bf16[256,640]{1,0:T(8,128)(2,1)S(1)}, u32[]{:S(2)}, u32[]{:S(2)}) collective-permute-start(bf16[256,640]{1,0:T(8,128)(2,1)S(1)} %get-tuple-element.10.refs_0_), channel_id=1, source_target_pairs={{0,1},{1,0},{2,3},{3,2},{4,5},{5,4},{6,7},{7,6}} | collective-permute-start | bytes 983048 | tf_op jit(solution)/shard_map/ppermute | solution.py:364
  286.5 6.6 %collective-permute-start = (bf16[128,640]{1,0:T(8,128)(2,1)S(1)}, bf16[128,640]{1,0:T(8,128)(2,1)S(1)}, u32[]{:S(2)}, u32[]{:S(2)}) collective-permute-start(bf16[128,640]{1,0:T(8,128)(2,1)S(1)} %get-tuple-element.9), channel_id=1, source_target_pairs={{0,2},{1,3},{2,0},{3,1},{4,6},{5,7},{6,4},{7,5}} | collective-permute-start | bytes 491528 | tf_op jit(solution)/shard_map/ppermute | solution.py:361
  293.1 10.1 %collective-permute-start.1 = (bf16[128,640]{1,0:T(8,128)(2,1)S(1)}, bf16[128,640]{1,0:T(8,128)(2,1)S(1)}, u32[]{:S(2)}, u32[]{:S(2)}) collective-permute-start(bf16[128,640]{1,0:T(8,128)(2,1)S(1)} %collective-permute-done.refs_0_), channel_id=1, source_target_pairs={{0,1},{1,0},{2,3},{3,2},{4,5},{5,4},{6,7},{7,6}} | collective-permute-start | bytes 491528 | tf_op jit(solution)/shard_map/ppermute | solution.py:364

commit v6 on v5

--- a/solution.py
+++ b/solution.py
@@ -12,16 +12,16 @@
 WIDTH = 640
 RING = 4
 SPLIT = 192
-PIECES = ((0, 0, 128, 0, 256), (0, 128, 128, 0, 256), (0, 0, 128, 256, 384), (0, 128, 128, 256, 384), (1, 0, 256, 0, 256), (1, 0, 256, 256, 384))
+PIECES = ((0, 0, 128, 0, 256), (0, 128, 128, 0, 256), (0, 0, 128, 256, 384), (0, 128, 128, 256, 384), (1, 0, 128, 0, 640), (1, 128, 128, 0, 640))
 LAST = 2
 TAIL = 128
 
 
 def kernel(
     a, g, out, got, la, lb, abuf, gbuf, sb1, rv1, total, sb2, rv2,
-    asem, hsem, gsem, g0sem, s1, r1, q1, s2, r2, s3, r3, s4, r4, s5, r5, s6, r6, turn,
+    asem, hsem, gsem, g0sem, ksem, s1, r1, q1, s2, r2, s3, r3, s4, r4, s5, r5, s6, r6, turn,
 ):
-    _, mats, _, dim = a.shape
+    _, mats, tokens, dim = a.shape
     quarter = dim // 4
     per = g.shape[3] // WIDTH
     chunks = mats * per
@@ -48,6 +48,14 @@
         part = rows(order[i], h * 128, 128)
         return pltpu.make_async_copy(a.at[0, 0, :, part], abuf.at[:, part], hsem.at[i // 2, h])
 
+    def load_first_a(j):
+        deep, part = pl.ds(j * (tokens // 2), tokens // 2), rows(order[0], 0, 128)
+        return pltpu.make_async_copy(a.at[0, 0, deep, part], abuf.at[deep, part], ksem.at[0, j])
+
+    def load_first_g(j):
+        deep, part = pl.ds(j * (tokens // 2), tokens // 2), pl.ds(0, 256)
+        return pltpu.make_async_copy(g.at[0, 0, deep, part], gbuf.at[0, deep, part], ksem.at[1, j])
+
     def load_g(k):
         return pltpu.make_async_copy(g.at[0, k // per, :, columns(k)], gbuf.at[k % 3], gsem.at[k % 3])
 
@@ -119,15 +127,23 @@
 
         for j, (k, r, h, c, w) in enumerate(PIECES):
             halves = [x for x in range(2) if k == 0 and r < (x + 1) * 128 and r + h > x * 128]
-            for x in halves:
-                need((0, x), load_half, 0, x)
-            if k == 0 and c < 256:
-                need("g", load_g0, 0, 0, 256)
+            if j == 0:
+                for d in range(2):
+                    load_first_a(d).wait()
+                    load_first_g(d).wait()
+                    deep = slice(d * (tokens // 2), (d + 1) * (tokens // 2))
+                    part = dot(abuf[deep, rows(order[0], 0, 128)], gbuf[0, deep, :256])
+                    total[:128, :256] = part if d == 0 else total[:128, :256] + part
+            elif k == 0:
+                for x in halves:
+                    if x:
+                        need((0, x), load_half, 0, x)
             if k == 0 and c + w > 256:
                 need("h", load_g0, 1, 256, 384)
             if k == 1:
                 need("k", load_g, 1)
-            sb1[k, 0, r:r + h, c:c + w] = piece(j, 0).astype(jnp.bfloat16)
+            own = total[:128, :256] if j == 0 else piece(j, 0)
+            sb1[k, 0, r:r + h, c:c + w] = own.astype(jnp.bfloat16)
             if j == 0:
                 pl.semaphore_wait(pltpu.get_barrier_semaphore(), 2)
             term_piece(j).start()
@@ -210,8 +226,9 @@
 
         give(k).start()
 
-    load_half(0, 0).start()
-    load_g0(0, 0, 256).start()
+    for j in range(2):
+        load_first_a(j).start()
+        load_first_g(j).start()
     load_half(2, 0).start()
     load_half(0, 1).start()
     load_half(2, 1).start()
@@ -345,7 +362,7 @@
                 pltpu.VMEM(block, f32),
                 pltpu.VMEM((2, *block), bf16),
                 pltpu.VMEM((RING, *block), bf16),
-                dma((4,)), dma((2, 2)), dma((3,)), dma((2,)),
+                dma((4,)), dma((2, 2)), dma((3,)), dma((2,)), dma((2, 2)),
                 dma((2, 2)), dma((2, 2)), dma((4,)),
                 dma((2,)), dma((RING,)),
                 dma((RING,)), dma((RING,)),

time: 304 us -> 304 us (level)
  no operation moved by 1% of the time
where the time goes in v6:
time: 304 us
  Pallas kernels  283 us (93%)
  waiting for transfers between devices  18.3 us (6%)
    pallas_call x1, Pallas kernels, step(): pl.pallas_call(kernel, out_shape=tuple((pltpu.VMEM(shape, bf16) for shape...  272 us
    ppermute x2, waiting for transfers between devices, across(): return lax.ppermute(x, 'dp', [(d, (d + 2) % 4) for d in range(4)])  18.3 us
    pallas_call x1, Pallas kernels, step(): pl.pallas_call(write, out_shape=jax.ShapeDtypeStruct((mats, dim, wide), b...  8.86 us
  transfers between devices with their start and end apart: 5, of which 2 were waited for; matrix products, arithmetic and copies ran while one was open for 0% of the time, Pallas kernels for 3%

profile of v6, /device:TPU:0, one launch (start us, length us, event | category | flops | bytes accessed | tf_op | source)
XLA Modules:
  0.0 303.7 jit_solution(17476591791707771046)
XLA Ops:
  0.0 272.0 %reduce.1 = (bf16[20,1024,640]{2,1,0:T(8,128)(2,1)S(1)}, bf16[256,640]{1,0:T(8,128)(2,1)S(1)}, bf16[384,640]{1,0:T(8,128)(2,1)S(1)}, bf16[128,640]{1,0:T(8,128)(2,1)S(1)}) custom-call(bf16[1,4,4096,1024]{3,2,1,0:T(8,128)(2,1)} %a.1, bf16[1,4,4096,3200]{3,2,1,0:T(8,128)(2,1)} %g.1), custom_call_target="tpu_custom_call" | custom-call | tf_op jit(solution)/shard_map/reduce/pallas_call | solution.py:351
  272.0 0.0 collective-permute-start.3
  272.1 11.7 %collective-permute-done.3.refs_2_ = bf16[384,640]{1,0:T(8,128)(2,1)S(1)} collective-permute-done((bf16[384,640]{1,0:T(8,128)(2,1)S(1)}, bf16[384,640]{1,0:T(8,128)(2,1)S(1)}, u32[]{:S(2)}, u32[]{:S(2)}) %collective-permute-start.3) | collective-permute-done | bytes 491552 | tf_op jit(solution)/shard_map/ppermute | solution.py:378
  283.8 2.2 collective-permute-start.4
  286.0 0.0 collective-permute-start.2
  286.0 0.0 collective-permute-start
  286.0 6.6 %collective-permute-done.refs_0_ = bf16[128,640]{1,0:T(8,128)(2,1)S(1)} collective-permute-done((bf16[128,640]{1,0:T(8,128)(2,1)S(1)}, bf16[128,640]{1,0:T(8,128)(2,1)S(1)}, u32[]{:S(2)}, u32[]{:S(2)}) %collective-permute-start) | collective-permute-done | bytes 163872 | tf_op jit(solution)/shard_map/ppermute | solution.py:378
  292.6 0.0 collective-permute-start.1
  292.6 8.9 %write.1.refs_4_ = bf16[4,1024,3200]{2,1,0:T(8,128)(2,1)} custom-call(bf16[20,1024,640]{2,1,0:T(8,128)(2,1)S(1)} %get-tuple-element.12.done), custom_call_target="tpu_custom_call" | custom-call | tf_op jit(solution)/shard_map/write/pallas_call | solution.py:397
  301.5 0.0 collective-permute-done.2.refs_1_
  301.5 0.0 collective-permute-done.4.refs_3_
  301.5 1.2 shard_map.28.refs_2_
  302.7 0.0 collective-permute-done.1.refs_1_
  302.7 0.8 shard_map.29
Async XLA Ops:
  272.0 11.7 %collective-permute-start.3 = (bf16[384,640]{1,0:T(8,128)(2,1)S(1)}, bf16[384,640]{1,0:T(8,128)(2,1)S(1)}, u32[]{:S(2)}, u32[]{:S(2)}) collective-permute-start(bf16[384,640]{1,0:T(8,128)(2,1)S(1)} %get-tuple-element.11), channel_id=1, source_target_pairs={{0,2},{1,3},{2,0},{3,1},{4,6},{5,7},{6,4},{7,5}} | collective-permute-start | bytes 1474568 | tf_op jit(solution)/shard_map/ppermute | solution.py:378
  283.8 17.7 %collective-permute-start.4 = (bf16[384,640]{1,0:T(8,128)(2,1)S(1)}, bf16[384,640]{1,0:T(8,128)(2,1)S(1)}, u32[]{:S(2)}, u32[]{:S(2)}) collective-permute-start(bf16[384,640]{1,0:T(8,128)(2,1)S(1)} %collective-permute-done.3.refs_2_), channel_id=1, source_target_pairs={{0,1},{1,0},{2,3},{3,2},{4,5},{5,4},{6,7},{7,6}} | collective-permute-start | bytes 1474568 | tf_op jit(solution)/shard_map/ppermute | solution.py:381
  286.0 15.5 %collective-permute-start.2 = (bf16[256,640]{1,0:T(8,128)(2,1)S(1)}, bf16[256,640]{1,0:T(8,128)(2,1)S(1)}, u32[]{:S(2)}, u32[]{:S(2)}) collective-permute-start(bf16[256,640]{1,0:T(8,128)(2,1)S(1)} %get-tuple-element.10.refs_0_), channel_id=1, source_target_pairs={{0,1},{1,0},{2,3},{3,2},{4,5},{5,4},{6,7},{7,6}} | collective-permute-start | bytes 983048 | tf_op jit(solution)/shard_map/ppermute | solution.py:381
  286.0 6.6 %collective-permute-start = (bf16[128,640]{1,0:T(8,128)(2,1)S(1)}, bf16[128,640]{1,0:T(8,128)(2,1)S(1)}, u32[]{:S(2)}, u32[]{:S(2)}) collective-permute-start(bf16[128,640]{1,0:T(8,128)(2,1)S(1)} %get-tuple-element.9), channel_id=1, source_target_pairs={{0,2},{1,3},{2,0},{3,1},{4,6},{5,7},{6,4},{7,5}} | collective-permute-start | bytes 491528 | tf_op jit(solution)/shard_map/ppermute | solution.py:378
  292.6 10.1 %collective-permute-start.1 = (bf16[128,640]{1,0:T(8,128)(2,1)S(1)}, bf16[128,640]{1,0:T(8,128)(2,1)S(1)}, u32[]{:S(2)}, u32[]{:S(2)}) collective-permute-start(bf16[128,640]{1,0:T(8,128)(2,1)S(1)} %collective-permute-done.refs_0_), channel_id=1, source_target_pairs={{0,1},{1,0},{2,3},{3,2},{4,5},{5,4},{6,7},{7,6}} | collective-permute-start | bytes 491528 | tf_op jit(solution)/shard_map/ppermute | solution.py:381

commit v7 on v6

--- a/solution.py
+++ b/solution.py
@@ -49,11 +49,11 @@
         return pltpu.make_async_copy(a.at[0, 0, :, part], abuf.at[:, part], hsem.at[i // 2, h])
 
     def load_first_a(j):
-        deep, part = pl.ds(j * (tokens // 2), tokens // 2), rows(order[0], 0, 128)
+        deep, part = pl.ds(j * (tokens // 4), tokens // 4), rows(order[0], 0, 128)
         return pltpu.make_async_copy(a.at[0, 0, deep, part], abuf.at[deep, part], ksem.at[0, j])
 
     def load_first_g(j):
-        deep, part = pl.ds(j * (tokens // 2), tokens // 2), pl.ds(0, 256)
+        deep, part = pl.ds(j * (tokens // 4), tokens // 4), pl.ds(0, 256)
         return pltpu.make_async_copy(g.at[0, 0, deep, part], gbuf.at[0, deep, part], ksem.at[1, j])
 
     def load_g(k):
@@ -128,10 +128,10 @@
         for j, (k, r, h, c, w) in enumerate(PIECES):
             halves = [x for x in range(2) if k == 0 and r < (x + 1) * 128 and r + h > x * 128]
             if j == 0:
-                for d in range(2):
+                for d in range(4):
                     load_first_a(d).wait()
                     load_first_g(d).wait()
-                    deep = slice(d * (tokens // 2), (d + 1) * (tokens // 2))
+                    deep = slice(d * (tokens // 4), (d + 1) * (tokens // 4))
                     part = dot(abuf[deep, rows(order[0], 0, 128)], gbuf[0, deep, :256])
                     total[:128, :256] = part if d == 0 else total[:128, :256] + part
             elif k == 0:
@@ -226,7 +226,7 @@
 
         give(k).start()
 
-    for j in range(2):
+    for j in range(4):
         load_first_a(j).start()
         load_first_g(j).start()
     load_half(2, 0).start()
@@ -362,7 +362,7 @@
                 pltpu.VMEM(block, f32),
                 pltpu.VMEM((2, *block), bf16),
                 pltpu.VMEM((RING, *block), bf16),
-                dma((4,)), dma((2, 2)), dma((3,)), dma((2,)), dma((2, 2)),
+                dma((4,)), dma((2, 2)), dma((3,)), dma((2,)), dma((2, 4)),
                 dma((2, 2)), dma((2, 2)), dma((4,)),
                 dma((2,)), dma((RING,)),
                 dma((RING,)), dma((RING,)),

time: 304 us -> 304 us (level)
  no operation moved by 1% of the time
where the time goes in v7:
time: 304 us
  Pallas kernels  283 us (93%)
  waiting for transfers between devices  18.3 us (6%)
    pallas_call x1, Pallas kernels, step(): pl.pallas_call(kernel, out_shape=tuple((pltpu.VMEM(shape, bf16) for shape...  272 us
    ppermute x2, waiting for transfers between devices, across(): return lax.ppermute(x, 'dp', [(d, (d + 2) % 4) for d in range(4)])  18.3 us
    pallas_call x1, Pallas kernels, step(): pl.pallas_call(write, out_shape=jax.ShapeDtypeStruct((mats, dim, wide), b...  8.86 us
  transfers between devices with their start and end apart: 5, of which 2 were waited for; matrix products, arithmetic and copies ran while one was open for 0% of the time, Pallas kernels for 3%

profile of v7, /device:TPU:0, one launch (start us, length us, event | category | flops | bytes accessed | tf_op | source)
XLA Modules:
  0.0 303.6 jit_solution(1229282392016208042)
XLA Ops:
  0.0 271.9 %reduce.1 = (bf16[20,1024,640]{2,1,0:T(8,128)(2,1)S(1)}, bf16[256,640]{1,0:T(8,128)(2,1)S(1)}, bf16[384,640]{1,0:T(8,128)(2,1)S(1)}, bf16[128,640]{1,0:T(8,128)(2,1)S(1)}) custom-call(bf16[1,4,4096,1024]{3,2,1,0:T(8,128)(2,1)} %a.1, bf16[1,4,4096,3200]{3,2,1,0:T(8,128)(2,1)} %g.1), custom_call_target="tpu_custom_call" | custom-call | tf_op jit(solution)/shard_map/reduce/pallas_call | solution.py:351
  271.9 0.0 collective-permute-start.3
  272.0 11.7 %collective-permute-done.3.refs_2_ = bf16[384,640]{1,0:T(8,128)(2,1)S(1)} collective-permute-done((bf16[384,640]{1,0:T(8,128)(2,1)S(1)}, bf16[384,640]{1,0:T(8,128)(2,1)S(1)}, u32[]{:S(2)}, u32[]{:S(2)}) %collective-permute-start.3) | collective-permute-done | bytes 491552 | tf_op jit(solution)/shard_map/ppermute | solution.py:378
  283.7 2.2 collective-permute-start.4
  285.9 0.0 collective-permute-start.2
  285.9 0.0 collective-permute-start
  285.9 6.6 %collective-permute-done.refs_0_ = bf16[128,640]{1,0:T(8,128)(2,1)S(1)} collective-permute-done((bf16[128,640]{1,0:T(8,128)(2,1)S(1)}, bf16[128,640]{1,0:T(8,128)(2,1)S(1)}, u32[]{:S(2)}, u32[]{:S(2)}) %collective-permute-start) | collective-permute-done | bytes 163872 | tf_op jit(solution)/shard_map/ppermute | solution.py:378
  292.5 0.0 collective-permute-start.1
  292.5 8.9 %write.1.refs_4_ = bf16[4,1024,3200]{2,1,0:T(8,128)(2,1)} custom-call(bf16[20,1024,640]{2,1,0:T(8,128)(2,1)S(1)} %get-tuple-element.12.done), custom_call_target="tpu_custom_call" | custom-call | tf_op jit(solution)/shard_map/write/pallas_call | solution.py:397
  301.4 0.0 collective-permute-done.2.refs_1_
  301.4 0.0 collective-permute-done.4.refs_3_
  301.4 1.2 shard_map.28.refs_2_
  302.6 0.0 collective-permute-done.1.refs_1_
  302.6 0.8 shard_map.29
Async XLA Ops:
  271.9 11.7 %collective-permute-start.3 = (bf16[384,640]{1,0:T(8,128)(2,1)S(1)}, bf16[384,640]{1,0:T(8,128)(2,1)S(1)}, u32[]{:S(2)}, u32[]{:S(2)}) collective-permute-start(bf16[384,640]{1,0:T(8,128)(2,1)S(1)} %get-tuple-element.11), channel_id=1, source_target_pairs={{0,2},{1,3},{2,0},{3,1},{4,6},{5,7},{6,4},{7,5}} | collective-permute-start | bytes 1474568 | tf_op jit(solution)/shard_map/ppermute | solution.py:378
  283.7 17.7 %collective-permute-start.4 = (bf16[384,640]{1,0:T(8,128)(2,1)S(1)}, bf16[384,640]{1,0:T(8,128)(2,1)S(1)}, u32[]{:S(2)}, u32[]{:S(2)}) collective-permute-start(bf16[384,640]{1,0:T(8,128)(2,1)S(1)} %collective-permute-done.3.refs_2_), channel_id=1, source_target_pairs={{0,1},{1,0},{2,3},{3,2},{4,5},{5,4},{6,7},{7,6}} | collective-permute-start | bytes 1474568 | tf_op jit(solution)/shard_map/ppermute | solution.py:381
  285.9 15.5 %collective-permute-start.2 = (bf16[256,640]{1,0:T(8,128)(2,1)S(1)}, bf16[256,640]{1,0:T(8,128)(2,1)S(1)}, u32[]{:S(2)}, u32[]{:S(2)}) collective-permute-start(bf16[256,640]{1,0:T(8,128)(2,1)S(1)} %get-tuple-element.10.refs_0_), channel_id=1, source_target_pairs={{0,1},{1,0},{2,3},{3,2},{4,5},{5,4},{6,7},{7,6}} | collective-permute-start | bytes 983048 | tf_op jit(solution)/shard_map/ppermute | solution.py:381
  285.9 6.6 %collective-permute-start = (bf16[128,640]{1,0:T(8,128)(2,1)S(1)}, bf16[128,640]{1,0:T(8,128)(2,1)S(1)}, u32[]{:S(2)}, u32[]{:S(2)}) collective-permute-start(bf16[128,640]{1,0:T(8,128)(2,1)S(1)} %get-tuple-element.9), channel_id=1, source_target_pairs={{0,2},{1,3},{2,0},{3,1},{4,6},{5,7},{6,4},{7,5}} | collective-permute-start | bytes 491528 | tf_op jit(solution)/shard_map/ppermute | solution.py:378
  292.5 10.1 %collective-permute-start.1 = (bf16[128,640]{1,0:T(8,128)(2,1)S(1)}, bf16[128,640]{1,0:T(8,128)(2,1)S(1)}, u32[]{:S(2)}, u32[]{:S(2)}) collective-permute-start(bf16[128,640]{1,0:T(8,128)(2,1)S(1)} %collective-permute-done.refs_0_), channel_id=1, source_target_pairs={{0,1},{1,0},{2,3},{3,2},{4,5},{5,4},{6,7},{7,6}} | collective-permute-start | bytes 491528 | tf_op jit(solution)/shard_map/ppermute | solution.py:381
